TPU v7x, 32 devices: a whole 2x2x4 slice. The times are simulated.
32 devices in a mesh: section: 2 (over y), dp: 4 (over x, core), mp: 4 (over z).
Axes of the slice: x: 2, y: 2, z: 4, core: 2. Of those that a mesh axis runs over, the one named last changes fastest.
Arguments:
- patches: bfloat16 [4096, 1280], P(('section', 'dp')), may hold values from -6 to 6
- patch_counts: int32 [16], P(('section', 'dp')), may hold values from 64 to 256, as said below
- dest_rows: int32 [1024], P(('section', 'dp')), may hold values from 0 to 4095, as said below
- qkv_weight: bfloat16 [1280, 3, 1280], P(None, None, 'mp'), may hold values from -1 to 1
- out_weight: bfloat16 [1280, 1280], P('mp'), may hold values from -0.15625 to 0.15625
- attn_gain: bfloat16 [1280], replicated, may hold values from 0.25 to 1.75
- merge_gain: bfloat16 [1280], replicated, may hold values from 0.25 to 1.75
- fc1_weight: bfloat16 [5120, 5120], P('mp', ('section', 'dp')), may hold values from -0.078125 to 0.078125
- fc1_bias: bfloat16 [5120], P(('section', 'dp')), may hold values from -3 to 3
- fc2_weight: bfloat16 [5120, 8192], P(('section', 'dp'), 'mp'), may hold values from -0.078125 to 0.078125
- fc2_bias: bfloat16 [8192], P('mp'), may hold values from -3 to 3
- text_embeds: bfloat16 [4096, 8192], P(('section', 'dp'), 'mp'), may hold values from -6 to 6
- section_hidden: bfloat16 [4096, 8192], P(('section', 'dp'), 'mp'), may hold values from -80 to 80
- llm_gain: bfloat16 [8192], P('mp'), may hold values from 0.25 to 1.75
Outputs:
- sequence_embeds: bfloat16 [4096, 8192], P(('section', 'dp'), 'mp')
- layer_inputs: bfloat16 [4096, 8192], P(('section', 'dp'), 'mp')
Inputs may be any that keep to these rules, and one draw needn't show every extreme that they name: `patch_counts`: multiples of 4; a tile's patches fill the first slots of its block. `dest_rows`: all rows differ. Each group's merged slots form runs of 16 consecutive slots (aligned); a run goes to one sequence slice (row // 512, numbered in section-major order), different runs of a group to different slices. Rows of slots that are not live are never written.
All inputs are finite; a program needn't handle non-finite values.
Results may differ from a plain program's by a relative error of at most 0.0055.
Values may be sent and summed in bfloat16 or wider, within the bound.
A program may use at most 128 MiB of HBM per device.

v0:
```python
import jax
import jax.numpy as jnp
from jax import lax
from jax.sharding import PartitionSpec as P

HEAD_DIM = 80
HID = 8192
vit_eps = 1e-06
llm_eps = 1e-06


def from_behind(value, axis, steps):
    count = lax.axis_size(axis)
    first, last = (max(0, -steps), min(count, count - steps))
    return lax.ppermute(value, axis, [(source, source + steps) for source in range(first, last)])


def layer_norm(values, gain):
    centred = values.astype(jnp.float32)
    centred = centred - jnp.mean(centred, axis=-1, keepdims=True)
    variance = jnp.mean(centred * centred, axis=-1, keepdims=True)
    return centred * lax.rsqrt(variance + vit_eps) * gain.astype(jnp.float32)


def sum_scatter_mp(blocks):
    return lax.psum_scatter(blocks, "mp", scatter_dimension=0, tiled=False).astype(jnp.float32)


def gather_mp(value):
    return lax.all_gather(value, "mp", axis=0, tiled=True)


def total_mp(value):
    return lax.psum(value, "mp")


def gather_groups(value):
    return lax.all_gather(value, ("section", "dp"), axis=0, tiled=True)


def sum_scatter_groups(value):
    return lax.psum_scatter(value, ("section", "dp"), scatter_dimension=0, tiled=True)


def per_device(
    patches,
    patch_counts,
    dest_rows,
    qkv_weight,
    out_weight,
    attn_gain,
    merge_gain,
    fc1_weight,
    fc1_bias,
    fc2_weight,
    fc2_bias,
    text_embeds,
    section_hidden,
    llm_gain,
):
    width = patches.shape[1]
    tile_total = patch_counts.shape[0]
    block_rows = patches.shape[0] // tile_total
    merged_rows = patches.shape[0] // 4
    local_cols = qkv_weight.shape[2]
    local_heads = local_cols // HEAD_DIM
    feature_cols = text_embeds.shape[1]
    seq_rows = text_embeds.shape[0]
    section_count = lax.axis_size("section")
    group_count = section_count * lax.axis_size("dp")
    run_cap = max(2, merged_rows // group_count)
    run_total = merged_rows // run_cap
    run_target = dest_rows.reshape(run_total, run_cap)[:, 0] // seq_rows
    takes = jnp.arange(group_count, dtype=jnp.int32)[:, None] == run_target[None, :]
    slot_in_tile = jnp.arange(merged_rows, dtype=jnp.int32) % (block_rows // 4)
    tile_counts = jnp.repeat(patch_counts, block_rows // 4, total_repeat_length=merged_rows)
    live = slot_in_tile * 4 < tile_counts
    place = jnp.where(live, dest_rows % seq_rows - seq_rows, 0).reshape(run_total, run_cap)
    send_place = jnp.sum(jnp.where(takes[:, :, None], place[None], 0), axis=1) + seq_rows
    got_place = lax.all_to_all(
        send_place, ("section", "dp"), split_axis=0, concat_axis=0, tiled=True
    )
    incoming = from_behind(section_hidden, "section", 1)
    normed_in = layer_norm(patches, attn_gain).astype(jnp.bfloat16)
    projections = jnp.dot(
        normed_in, qkv_weight.reshape(width, 3 * local_cols), preferred_element_type=jnp.float32
    ).astype(jnp.bfloat16)
    projections = projections.reshape(tile_total, block_rows, 3, local_heads, HEAD_DIM)
    query_part = projections[:, :, 0]
    key_part = projections[:, :, 1]
    value_part = projections[:, :, 2]
    scores = jnp.einsum(
        "tqhd,tkhd->thqk", query_part, key_part, preferred_element_type=jnp.float32
    ) * HEAD_DIM ** (-0.5)
    key_live = (
        jnp.arange(block_rows, dtype=jnp.int32)[None, None, None, :]
        < patch_counts[:, None, None, None]
    )
    scores = jnp.where(key_live, scores, -1e30)
    weights = jax.nn.softmax(scores, axis=-1).astype(jnp.bfloat16)
    attended = jnp.einsum(
        "thqk,tkhd->tqhd", weights, value_part, preferred_element_type=jnp.float32
    ).astype(jnp.bfloat16)
    attended = attended.reshape(patches.shape[0], local_cols)
    partial_proj = jnp.dot(attended, out_weight, preferred_element_type=jnp.float32)
    position = lax.axis_index("mp")
    own_patch = lax.dynamic_slice_in_dim(
        patches.reshape(merged_rows, 4, width), position, 1, 1
    ).reshape(merged_rows, width)
    own_proj = sum_scatter_mp(
        partial_proj.astype(jnp.bfloat16).reshape(merged_rows, 4, width).transpose(1, 0, 2)
    )
    block_out = (own_patch.astype(jnp.float32) + own_proj).astype(jnp.bfloat16)
    merge_part = layer_norm(block_out, merge_gain).astype(jnp.bfloat16)
    lane_same = jnp.arange(run_cap)[:, None] == jnp.arange(run_cap)[None, :]
    order = (takes[:, None, :, None] & lane_same[None, :, None, :]).reshape(
        group_count * run_cap, merged_rows
    )
    merge_part = jnp.dot(
        order.astype(jnp.bfloat16), merge_part, preferred_element_type=jnp.float32
    ).astype(jnp.bfloat16)
    slot_rows = group_count * run_cap
    gathered = gather_groups(merge_part)
    gathered = (
        gathered.reshape(group_count, group_count, run_cap, width)
        .transpose(1, 0, 2, 3)
        .reshape(group_count * slot_rows, width)
    )
    first_partial = jnp.dot(gathered, fc1_weight, preferred_element_type=jnp.float32)
    mp_count = lax.axis_size("mp")
    first_total = sum_scatter_mp(
        first_partial.astype(jnp.bfloat16).reshape(mp_count, -1, fc1_weight.shape[1])
    )
    hidden_part = jax.nn.gelu(first_total + fc1_bias.astype(jnp.float32), approximate=False).astype(
        jnp.bfloat16
    )
    hidden = gather_mp(hidden_part)
    second_partial = jnp.dot(hidden, fc2_weight, preferred_element_type=jnp.float32)
    embed_total = sum_scatter_groups(second_partial.astype(jnp.bfloat16)).astype(jnp.float32)
    image_embeds = (embed_total + fc2_bias.astype(jnp.float32)).astype(jnp.bfloat16)
    hits = got_place.reshape(1, -1) == jnp.arange(seq_rows, dtype=jnp.int32)[:, None]
    placed = jnp.dot(
        hits.astype(jnp.bfloat16), image_embeds, preferred_element_type=jnp.float32
    ).astype(jnp.bfloat16)
    sequence_embeds = jnp.where(jnp.any(hits, axis=1)[:, None], placed, text_embeds)
    entering = jnp.where(lax.axis_index("section") == 0, sequence_embeds, incoming).astype(
        jnp.float32
    )
    row_total = total_mp(jnp.sum(entering * entering, axis=1))
    layer_inputs = (
        entering * lax.rsqrt(row_total / HID + llm_eps)[:, None] * llm_gain.astype(jnp.float32)
    ).astype(jnp.bfloat16)
    return (sequence_embeds, layer_inputs)


def solution(mesh):
    in_specs = (
        P(("section", "dp"), None),
        P(("section", "dp")),
        P(("section", "dp")),
        P(None, None, "mp"),
        P("mp", None),
        P(),
        P(),
        P("mp", ("section", "dp")),
        P(("section", "dp")),
        P(("section", "dp"), "mp"),
        P("mp"),
        P(("section", "dp"), "mp"),
        P(("section", "dp"), "mp"),
        P("mp"),
    )
    out_specs = (P(("section", "dp"), "mp"), P(("section", "dp"), "mp"))
    return jax.shard_map(
        per_device, mesh=mesh, in_specs=in_specs, out_specs=out_specs, check_vma=False
    )
```

profile of v0, /device:TPU:4, one launch (start us, length us, event | category | flops | bytes accessed | tf_op | source)
XLA Modules:
  0.0 269.9 jit_solution(1609884030651612214)
XLA Ops:
  7.2 1.7 convert_reduce_fusion
  9.0 0.1 copy-done.1
  9.1 0.5 fusion.7
  9.6 4.3 %convolution_convert_fusion.5 = bf16[512,960]{0,1:T(8,128)(2,1)} fusion(bf16[1280,960]{0,1:T(8,128)(2,1)} %bitcast.95, bf16[512,1280]{1,0:T(8,128)(2,1)S(1)} %copy-done.1, f32[1280]{0:T(1024)S(1)} %convert_element_type.118, f32[512]{0:T(512)S(1)} %add_rsqrt_fusion.1, f32[512]{0:T(512)S(1)} %broadcast_multiply_fusion), kind=kOutput, calls=%fused_computation.24 | convolution fusion | flops 1262059520 | bytes 4760576 | tf_op jit(solution)/shard_map/dot_general | solution.py:85
  13.9 3.3 %reshape.265 = bf16[2,256,3,4,80]{1,0,4,3,2:T(2,128)(2,1)} reshape(bf16[512,960]{0,1:T(8,128)(2,1)} %convolution_convert_fusion.5) | data formatting | bytes 1966080 | tf_op jit(solution)/shard_map/reshape | solution.py:88
  17.2 2.7 %fusion.71 = (bf16[2,256,1,4,80]{1,0,4,3,2:T(2,128)(2,1)S(1)}, bf16[2,256,1,4,80]{1,0,4,3,2:T(2,128)(2,1)S(1)}, bf16[2,256,1,4,80]{1,0,4,3,2:T(2,128)(2,1)}) fusion(bf16[2,256,3,4,80]{1,0,4,3,2:T(2,128)(2,1)} %reshape.265), kind=kLoop, calls=%fused_computation.118 | loop fusion | bytes 1966080 | tf_op jit(solution)/shard_map/slice | solution.py:91
  19.9 0.1 iota_compare_fusion.4
  19.9 3.2 %fusion.73 = (f32[2,4,256]{2,1,0:T(4,128)S(1)}, f32[2,4,256,256]{2,3,1,0:T(8,128)}) fusion(pred[2,256]{1,0:T(4,128)(4,1)S(1)} %iota_compare_fusion.4, bf16[2,256,1,4,80]{1,0,4,3,2:T(2,128)(2,1)} %get-tuple-element.16, bf16[2,256,1,4,80]{1,0,4,3,2:T(2,128)(2,1)S(1)} %get-tuple-element.15), kind=kOutput, calls=%fused_computation.120 | convolution fusion | flops 85983488 | bytes 2761216 | tf_op jit(solution)/shard_map/sub | solution.py:100
  23.1 2.0 fusion.15
  25.1 0.3 copy.50
  25.5 1.9 convolution_convert_fusion.2
  27.4 3.5 %reshape.267 = bf16[128,4,1280]{2,1,0:T(4,128)(2,1)} reshape(bf16[512,1280]{1,0:T(8,128)(2,1)} %convolution_convert_fusion.2) | data formatting | bytes 2621440 | tf_op jit(solution)/shard_map/reshape | solution.py:111
  30.9 2.5 copy.92
  33.4 0.0 all-gather.3.cloned.1.call-start
  33.5 3.5 %reshape.263 = bf16[128,4,1280]{2,1,0:T(4,128)(2,1)} reshape(bf16[512,1280]{1,0:T(8,128)(2,1)} %param.16) | data formatting | bytes 2621440 | tf_op jit(solution)/shard_map/reshape | solution.py:108
  37.0 0.1 reshape.262
  37.1 0.1 slice_reduce_fusion
  37.2 0.1 broadcast_and_fusion
  37.4 0.2 and.61
  37.6 1.9 dynamic-slice_convert_fusion
  39.5 26.6 %reduce-scatter.4.cloned.1.call-done = bf16[1,128,1280]{2,1,0:T(8,128)(2,1)} async-done(((bf16[4,128,1280]{2,1,0:T(8,128)(2,1)}), bf16[1,128,1280]{2,1,0:T(8,128)(2,1)}) %reduce-scatter.4.cloned.1.call-update) | async-done | bytes 327696 | tf_op jit(solution)/shard_map/reduce_scatter | solution.py:26
  66.2 1.2 convert_reduce_fusion.1
  67.4 1.2 fusion.20
  68.6 1.1 convolution_convert_fusion.3
  69.7 28.7 %all-gather.3.cloned.1.call-done = bf16[1024,1280]{1,0:T(8,128)(2,1)} async-done(((bf16[128,1280]{1,0:T(8,128)(2,1)}), bf16[1024,1280]{1,0:T(8,128)(2,1)}) %all-gather.3.cloned.1.call-update) | async-done | bytes 2621456 | tf_op jit(solution)/shard_map/all_gather | solution.py:38
  98.4 2.1 copy.53
  100.5 0.1 copy-done.11
  100.6 3.3 %convolution_convert_fusion.4 = bf16[1024,640]{1,0:T(8,128)(2,1)} fusion(bf16[1024,1280]{1,0:T(8,128)(2,1)S(1)} %bitcast.91, bf16[1280,640]{1,0:T(8,128)(2,1)S(1)} %copy-done.11), kind=kOutput, calls=%fused_computation.23 | convolution fusion | flops 1678376960 | bytes 5570560 | tf_op jit(solution)/shard_map/dot_general | solution.py:129
  103.9 0.2 all-gather.5.cloned.1.call-start
  104.1 31.3 %reduce-scatter.6.cloned.1.call-done = bf16[1,256,640]{2,1,0:T(8,128)(2,1)} async-done(((bf16[4,256,640]{2,1,0:T(8,128)(2,1)}), bf16[1,256,640]{2,1,0:T(8,128)(2,1)}) %reduce-scatter.6.cloned.1.call-update) | async-done | bytes 327696 | tf_op jit(solution)/shard_map/reduce_scatter | solution.py:26
  135.5 3.2 %fusion.27 = bf16[256,640]{1,0:T(8,128)(2,1)} fusion(bf16[1,256,640]{2,1,0:T(8,128)(2,1)} %reduce-scatter.6.cloned.1.call-done, f32[640]{0:T(1024)S(1)} %convert_element_type.142), kind=kLoop, calls=%fused_computation.48 | loop fusion | flops 10977280 | bytes 657920 | tf_op jit(solution)/shard_map/convert_element_type | solution.py:134
  138.7 31.3 %all-gather.5.cloned.1.call-done = bf16[1024,640]{1,0:T(8,128)(2,1)} async-done(((bf16[256,640]{1,0:T(8,128)(2,1)}), bf16[1024,640]{1,0:T(8,128)(2,1)}) %all-gather.5.cloned.1.call-update) | async-done | bytes 1310736 | tf_op jit(solution)/shard_map/all_gather | solution.py:30
  170.0 6.3 %convolution_convert_fusion = bf16[1024,2048]{1,0:T(8,128)(2,1)} fusion(bf16[1024,640]{1,0:T(8,128)(2,1)} %all-gather.5.cloned.1.call-done, bf16[640,2048]{1,0:T(8,128)(2,1)S(1)} %copy-done), kind=kOutput, calls=%fused_computation.6 | convolution fusion | flops 2686451712 | bytes 8126464 | tf_op jit(solution)/shard_map/dot_general | solution.py:138
  176.3 1.4 collective-permute-start
  177.8 0.6 fusion.72
  178.3 1.3 compare_select_fusion.2
  179.6 0.1 broadcast_in_dim.46
  179.7 0.1 select_reduce_fusion
  179.8 0.6 broadcast_add_fusion
  180.4 7.2 %all-to-all-start = ((s32[8,1,16]{2,1,0:T(1,128)}), s32[8,1,16]{2,1,0:T(1,128)S(1)}, u32[]{:S(2)}, u32[]{:S(2)}) async-start(s32[8,1,16]{2,1,0:T(1,128)} %bitcast.3), calls=%async_computation | async-start | bytes 8192 | tf_op jit(solution)/shard_map/all_to_all | solution.py:80
  187.7 54.5 %all-to-all-done = s32[8,1,16]{2,1,0:T(1,128)S(1)} async-done(((s32[8,1,16]{2,1,0:T(1,128)}), s32[8,1,16]{2,1,0:T(1,128)S(1)}, u32[]{:S(2)}, u32[]{:S(2)}) %all-to-all-start) | async-done | bytes 544 | tf_op jit(solution)/shard_map/all_to_all | solution.py:80
  242.2 0.5 broadcast.236
  242.7 0.7 reduce.7
  243.4 0.1 eq.62
  243.5 0.2 fusion.64
  243.7 4.9 %fusion.1 = (f32[512]{0:T(512)S(1)}, bf16[512,2048]{1,0:T(8,128)(2,1)}) fusion(bf16[512,2048]{1,0:T(8,128)(2,1)} %collective-permute-done, pred[]{:T(512)S(6)} %eq.69, bf16[512,2048]{1,0:T(8,128)(2,1)} %param.27, bf16[128,2048]{1,0:T(8,128)(2,1)} %reduce-scatter.8.cloned.1.call-done, f32[2048]{0:T(1024)S(1)} %convert_element_type.146, s32[128]{0:T(128)S(1)} %eq.62, ...), kind=kOutput, calls=%fused_computation.3 | convolution fusion | flops 275578368 | bytes 6827009 | tf_op jit(solution)/shard_map/dot_general | solution.py:142
  248.6 10.7 %psum.7 = f32[512]{0:T(512)S(1)} all-reduce(f32[512]{0:T(512)S(1)} %get-tuple-element.21), channel_id=1, replica_groups=mesh['section'=2,'dp'=4,'mp'=4] {'mp'}, use_global_device_ids=true, to_apply=%region_12.13 | all-reduce | flops 512 | bytes 4096 | tf_op jit(solution)/shard_map/psum | solution.py:34
  259.2 4.1 %fusion.3 = bf16[512,2048]{1,0:T(8,128)(2,1)} fusion(f32[2048]{0:T(1024)S(1)} %convert_element_type.150, f32[512]{0:T(512)S(1)} %add_rsqrt_fusion, bf16[512,2048]{1,0:T(8,128)(2,1)} %get-tuple-element.22, bf16[512,2048]{1,0:T(8,128)(2,1)} %collective-permute-done, pred[]{:T(512)S(6)} %eq.69), kind=kLoop, calls=%fused_computation.5 | loop fusion | flops 5242880 | bytes 6301697 | tf_op jit(solution)/shard_map/convert_element_type | solution.py:152
  (48 shorter events, 0.4 us)
Async XLA Ops:
  7.2 162.9 %copy-start = (bf16[640,2048]{1,0:T(8,128)(2,1)S(1)}, bf16[640,2048]{1,0:T(8,128)(2,1)}, u32[]{:S(2)}) copy-start(bf16[640,2048]{1,0:T(8,128)(2,1)} %param.25) | copy-start | bytes 7864324
  7.2 2.4 copy-start.3
  7.2 59.0 %reduce-scatter.4.cloned.1.call-start = ((), (), s32[]{:S(2)}) async-start(), calls=%async_computation.4 | async-start | bytes 1638400 | tf_op jit(solution)/shard_map/reduce_scatter | solution.py:26
  7.2 1.9 copy-start.1
  13.9 6.0 %copy-start.9 = (s32[2]{0:T(128)S(1)}, s32[2]{0:T(128)}, u32[]{:S(2)}) copy-start(s32[2]{0:T(128)} %param.17) | copy-start | bytes 28
  23.1 2.4 copy-start.12
  33.4 3.6 %copy-start.8 = (s32[128]{0:T(128)S(1)}, s32[128]{0:T(128)}, u32[]{:S(2)}) copy-start(s32[128]{0:T(128)} %param.18) | copy-start | bytes 1540
  33.4 4.2 %copy-start.4 = (bf16[1280]{0:T(1024)(128)(2,1)S(1)}, bf16[1280]{0:T(1024)(128)(2,1)}, u32[]{:S(2)}) copy-start(bf16[1280]{0:T(1024)(128)(2,1)} %param.22) | copy-start | bytes 7684
  33.4 65.0 %all-gather.3.cloned.1.call-start = ((), (), s32[]{:S(2)}) async-start(), calls=%async_computation.5 | async-start | bytes 2949120 | tf_op jit(solution)/shard_map/all_gather | solution.py:38
  66.2 2.4 copy-start.2
  69.7 65.8 %reduce-scatter.6.cloned.1.call-start = ((), (), s32[]{:S(2)}) async-start(), calls=%async_computation.6 | async-start | bytes 1638400 | tf_op jit(solution)/shard_map/reduce_scatter | solution.py:26
  98.4 2.2 copy-start.11
  100.6 3.5 %copy-start.7 = (bf16[640]{0:T(1024)(128)(2,1)S(1)}, bf16[640]{0:T(1024)(128)(2,1)}, u32[]{:S(2)}) copy-start(bf16[640]{0:T(1024)(128)(2,1)} %param.24) | copy-start | bytes 3844
  103.9 66.1 %all-gather.5.cloned.1.call-start = ((), (), s32[]{:S(2)}) async-start(), calls=%async_computation.7 | async-start | bytes 1638400 | tf_op jit(solution)/shard_map/all_gather | solution.py:30
  138.7 105.0 %reduce-scatter.8.cloned.1.call-start = ((), (), s32[]{:S(2)}) async-start(), calls=%async_computation.8 | async-start | bytes 4718592 | tf_op jit(solution)/shard_map/reduce_scatter | solution.py:42
  176.3 2.0 copy-start.10
  176.3 11.3 %copy-start.5 = (bf16[2048]{0:T(1024)(128)(2,1)S(1)}, bf16[2048]{0:T(1024)(128)(2,1)}, u32[]{:S(2)}) copy-start(bf16[2048]{0:T(1024)(128)(2,1)} %param.26) | copy-start | bytes 12292
  176.3 11.4 %copy-start.6 = (bf16[2048]{0:T(1024)(128)(2,1)S(1)}, bf16[2048]{0:T(1024)(128)(2,1)}, u32[]{:S(2)}) copy-start(bf16[2048]{0:T(1024)(128)(2,1)} %param.29) | copy-start | bytes 12292
  176.3 67.3 %collective-permute-start = (bf16[512,2048]{1,0:T(8,128)(2,1)}, bf16[512,2048]{1,0:T(8,128)(2,1)}, u32[]{:S(2)}, u32[]{:S(2)}) collective-permute-start(bf16[512,2048]{1,0:T(8,128)(2,1)} %param.28), channel_id=1, source_target_pairs={{0,16},{1,17},{2,18},{3,19},{4,20},{5,21},{6,22},{7,23},{8,24},{9,... | collective-permute-start | bytes 6291464 | tf_op jit(solution)/shard_map/ppermute | solution.py:15
  180.4 61.8 %all-to-all-start = ((s32[8,1,16]{2,1,0:T(1,128)}), s32[8,1,16]{2,1,0:T(1,128)S(1)}, u32[]{:S(2)}, u32[]{:S(2)}) async-start(s32[8,1,16]{2,1,0:T(1,128)} %bitcast.3), calls=%async_computation | async-start | bytes 8192 | tf_op jit(solution)/shard_map/all_to_all | solution.py:80
Sparse Core Ops, SparseCore 0:
  33.6 32.5 reduce-scatter.3
  69.8 28.5 all-gather.2
  104.0 31.4 reduce-scatter.5
  138.8 31.1 all-gather.4
  176.4 65.5 reduce-scatter.7
where the time goes:
time: 271 us; the launch traced here: 270 us
  waiting for transfers between devices  173 us (64%)
  matrix products  26.9 us (10%)
  local copies, waits for them, and re-layouts  19.9 us (7%)
  other arithmetic  16.9 us (6%)
  between operations  14 us (5%)
  blocking collectives  10.7 us (4%)
  starting transfers between devices  9.03 us (3%)
    reduce_scatter x2, waiting for transfers between devices, sum_scatter_mp(): lax.psum_scatter(blocks, 'mp', scatter_dimension=0, tiled=False)  58 us
    all_to_all x1, waiting for transfers between devices, per_device(): lax.all_to_all(send_place, ('section', 'dp'), split_axis=0, concat_axis=0...  54.5 us
    all_gather x1, waiting for transfers between devices, gather_mp(): return lax.all_gather(value, 'mp', axis=0, tiled=True)  31.3 us
    all_gather x1, waiting for transfers between devices, gather_groups(): return lax.all_gather(value, ('section', 'dp'), axis=0, tiled=True)  28.7 us
    psum x1, blocking collectives, total_mp(): return lax.psum(value, 'mp')  10.7 us
    all_to_all x1, starting transfers between devices, per_device(): lax.all_to_all(send_place, ('section', 'dp'), split_axis=0, concat_axis=0...  7.22 us
    dot_general x1, matrix products, per_device(): jnp.dot(hidden, fc2_weight, preferred_element_type=jnp.float32)  6.27 us
    reshape x2, local copies, waits for them, and re-layouts, per_device(): partial_proj.astype(jnp.bfloat16).reshape(merged_rows, 4, width)  5.99 us
  transfers between devices with their start and end apart: 7, of which 5 were waited for; matrix products, arithmetic and copies ran while one was open for 4% of the time, Pallas kernels for 0%

commit v1 on v0

--- a/solution.py
+++ b/solution.py
@@ -7,6 +7,18 @@
 HID = 8192
 vit_eps = 1e-06
 llm_eps = 1e-06
+
+
+def gather_by_bits(x, axis, dim):
+    ways, here = (lax.axis_size(axis), lax.axis_index(axis))
+    grown, reach = (x, 1)
+    while reach < ways:
+        theirs = lax.ppermute(grown, axis, [(d, d ^ reach) for d in range(ways)])
+        mine_first = jnp.concatenate([grown, theirs], axis=dim)
+        theirs_first = jnp.concatenate([theirs, grown], axis=dim)
+        grown = jnp.where(here & reach == 0, mine_first, theirs_first)
+        reach = 2 * reach
+    return grown
 
 
 def from_behind(value, axis, steps):
@@ -35,7 +47,7 @@
 
 
 def gather_groups(value):
-    return lax.all_gather(value, ("section", "dp"), axis=0, tiled=True)
+    return gather_by_bits(value, ("section", "dp"), 0)
 
 
 def sum_scatter_groups(value):

time: 271 us -> 296 us (1.092)
  waiting for transfers between devices: 173 us -> 190 us
  other arithmetic: 16.9 us -> 23.9 us
    ppermute x0 -> x3, waiting for transfers between devices: none -> 47.1 us  [gather_by_bits(): theirs = lax.ppermute(grown, axis, [(d, d ^ reach) for d in range(ways)])]
    all_gather x1 -> x0, waiting for transfers between devices: 28.7 us -> none  [gather_groups(): return lax.all_gather(value, ('section', 'dp'), axis=0, tiled=True)]
    select_n x0 -> x3, other arithmetic: none -> 7.02 us  [gather_by_bits(): grown = jnp.where(here & reach == 0, mine_first, theirs_first)]
  transfers between devices with their start and end apart: 7 -> 9, of which waited for: 5 -> 7; matrix products, arithmetic and copies ran while one was open for 4% -> 3% of each run, Pallas kernels for 0% -> 0%
where the time goes in v1:
time: 296 us; the launch traced here: 295 us
  waiting for transfers between devices  190 us (64%)
  matrix products  26.9 us (9%)
  other arithmetic  23.9 us (8%)
  local copies, waits for them, and re-layouts  19.1 us (6%)
  between operations  14 us (5%)
  starting transfers between devices  11.1 us (4%)
  blocking collectives  10.7 us (4%)
    reduce_scatter x2, waiting for transfers between devices, sum_scatter_mp(): lax.psum_scatter(blocks, 'mp', scatter_dimension=0, tiled=False)  56.6 us
    all_to_all x1, waiting for transfers between devices, per_device(): lax.all_to_all(send_place, ('section', 'dp'), split_axis=0, concat_axis=0...  54.5 us
    ppermute x3, waiting for transfers between devices, gather_by_bits(): theirs = lax.ppermute(grown, axis, [(d, d ^ reach) for d in range(ways)])  47.1 us
    all_gather x1, waiting for transfers between devices, gather_mp(): return lax.all_gather(value, 'mp', axis=0, tiled=True)  31.3 us
    psum x1, blocking collectives, total_mp(): return lax.psum(value, 'mp')  10.7 us
    all_to_all x1, starting transfers between devices, per_device(): lax.all_to_all(send_place, ('section', 'dp'), split_axis=0, concat_axis=0...  7.22 us
    select_n x3, other arithmetic, gather_by_bits(): grown = jnp.where(here & reach == 0, mine_first, theirs_first)  7.02 us
    dot_general x1, matrix products, per_device(): jnp.dot(hidden, fc2_weight, preferred_element_type=jnp.float32)  6.27 us
  transfers between devices with their start and end apart: 9, of which 7 were waited for; matrix products, arithmetic and copies ran while one was open for 3% of the time, Pallas kernels for 0%

profile of v1, /device:TPU:4, one launch (start us, length us, event | category | flops | bytes accessed | tf_op | source)
XLA Modules:
  0.0 295.2 jit_solution(18223835804257184597)
XLA Ops:
  7.2 1.7 convert_reduce_fusion
  9.0 0.1 copy-done.1
  9.1 0.5 fusion.7
  9.6 4.3 %convolution_convert_fusion.5 = bf16[512,960]{0,1:T(8,128)(2,1)} fusion(bf16[1280,960]{0,1:T(8,128)(2,1)} %bitcast.95, bf16[512,1280]{1,0:T(8,128)(2,1)S(1)} %copy-done.1, f32[1280]{0:T(1024)S(1)} %convert_element_type.118, f32[512]{0:T(512)S(1)} %add_rsqrt_fusion.1, f32[512]{0:T(512)S(1)} %broadcast_multiply_fusion), kind=kOutput, calls=%fused_computation.25 | convolution fusion | flops 1262059520 | bytes 4760576 | tf_op jit(solution)/shard_map/dot_general | solution.py:97
  13.9 3.3 %reshape.267 = bf16[2,256,3,4,80]{1,0,4,3,2:T(2,128)(2,1)} reshape(bf16[512,960]{0,1:T(8,128)(2,1)} %convolution_convert_fusion.5) | data formatting | bytes 1966080 | tf_op jit(solution)/shard_map/reshape | solution.py:100
  17.2 2.7 fusion.71
  19.9 3.2 %fusion.73 = (f32[2,4,256]{2,1,0:T(4,128)S(1)}, f32[2,4,256,256]{2,3,1,0:T(8,128)}) fusion(pred[2,256]{1,0:T(4,128)(4,1)S(1)} %iota_compare_fusion.4, bf16[2,256,1,4,80]{1,0,4,3,2:T(2,128)(2,1)} %get-tuple-element.16, bf16[2,256,1,4,80]{1,0,4,3,2:T(2,128)(2,1)S(1)} %get-tuple-element.15), kind=kOutput, calls=%fused_computation.123 | convolution fusion | flops 85983488 | bytes 2761216 | tf_op jit(solution)/shard_map/sub | solution.py:112
  23.1 2.0 fusion.15
  25.1 0.3 copy.50
  25.5 1.9 convolution_convert_fusion.2
  27.4 3.5 %reshape.269 = bf16[128,4,1280]{2,1,0:T(4,128)(2,1)} reshape(bf16[512,1280]{1,0:T(8,128)(2,1)} %convolution_convert_fusion.2) | data formatting | bytes 2621440 | tf_op jit(solution)/shard_map/reshape | solution.py:123
  30.9 2.5 copy.92
  33.4 0.2 reduce-scatter.6.cloned.1.call-start
  33.7 3.5 %reshape.265 = bf16[128,4,1280]{2,1,0:T(4,128)(2,1)} reshape(bf16[512,1280]{1,0:T(8,128)(2,1)} %param.16) | data formatting | bytes 2621440 | tf_op jit(solution)/shard_map/reshape | solution.py:120
  37.4 0.1 broadcast_and_fusion
  37.5 0.2 and.74
  37.8 1.9 dynamic-slice_convert_fusion
  39.7 26.4 %reduce-scatter.4.cloned.1.call-done = bf16[1,128,1280]{2,1,0:T(8,128)(2,1)} async-done(((bf16[4,128,1280]{2,1,0:T(8,128)(2,1)}), bf16[1,128,1280]{2,1,0:T(8,128)(2,1)}) %reduce-scatter.4.cloned.1.call-update) | async-done | bytes 327696 | tf_op jit(solution)/shard_map/reduce_scatter | solution.py:38
  66.2 1.2 convert_reduce_fusion.1
  67.4 1.2 fusion.20
  68.6 1.1 convolution_convert_fusion.3
  69.6 2.0 collective-permute-done
  71.6 1.4 maximum_select_fusion.2
  73.0 1.5 collective-permute-start.1
  74.6 15.4 %collective-permute-done.1 = bf16[256,1280]{1,0:T(8,128)(2,1)} collective-permute-done((bf16[256,1280]{1,0:T(8,128)(2,1)S(1)}, bf16[256,1280]{1,0:T(8,128)(2,1)}, u32[]{:S(2)}, u32[]{:S(2)}) %collective-permute-start.1) | collective-permute-done | bytes 655392 | tf_op jit(solution)/shard_map/ppermute | solution.py:16
  90.0 2.7 maximum_select_fusion.1
  92.7 0.5 collective-permute-start.2
  93.2 29.7 %collective-permute-done.2 = bf16[512,1280]{1,0:T(8,128)(2,1)} collective-permute-done((bf16[512,1280]{1,0:T(8,128)(2,1)}, bf16[512,1280]{1,0:T(8,128)(2,1)}, u32[]{:S(2)}, u32[]{:S(2)}) %collective-permute-start.2) | collective-permute-done | bytes 1310752 | tf_op jit(solution)/shard_map/ppermute | solution.py:16
  122.9 2.9 maximum_select_fusion
  125.9 0.2 copy.53
  126.1 1.2 copy-done.11
  127.3 3.3 %convolution_convert_fusion.4 = bf16[1024,640]{1,0:T(8,128)(2,1)} fusion(bf16[1024,1280]{1,0:T(8,128)(2,1)S(1)} %bitcast.91, bf16[1280,640]{1,0:T(8,128)(2,1)S(1)} %copy-done.11), kind=kOutput, calls=%fused_computation.24 | convolution fusion | flops 1678376960 | bytes 5570560 | tf_op jit(solution)/shard_map/dot_general | solution.py:141
  130.7 30.1 %reduce-scatter.6.cloned.1.call-done = bf16[1,256,640]{2,1,0:T(8,128)(2,1)} async-done(((bf16[4,256,640]{2,1,0:T(8,128)(2,1)}), bf16[1,256,640]{2,1,0:T(8,128)(2,1)}) %reduce-scatter.6.cloned.1.call-update) | async-done | bytes 327696 | tf_op jit(solution)/shard_map/reduce_scatter | solution.py:38
  160.8 3.2 %fusion.27 = bf16[256,640]{1,0:T(8,128)(2,1)} fusion(bf16[1,256,640]{2,1,0:T(8,128)(2,1)} %reduce-scatter.6.cloned.1.call-done, f32[640]{0:T(1024)S(1)} %convert_element_type.142), kind=kLoop, calls=%fused_computation.50 | loop fusion | flops 10977280 | bytes 657920 | tf_op jit(solution)/shard_map/convert_element_type | solution.py:146
  164.0 31.3 %all-gather.2.cloned.1.call-done = bf16[1024,640]{1,0:T(8,128)(2,1)} async-done(((bf16[256,640]{1,0:T(8,128)(2,1)}), bf16[1024,640]{1,0:T(8,128)(2,1)}) %all-gather.2.cloned.1.call-update) | async-done | bytes 1310736 | tf_op jit(solution)/shard_map/all_gather | solution.py:42
  195.3 6.3 %convolution_convert_fusion = bf16[1024,2048]{1,0:T(8,128)(2,1)} fusion(bf16[1024,640]{1,0:T(8,128)(2,1)} %all-gather.2.cloned.1.call-done, bf16[640,2048]{1,0:T(8,128)(2,1)S(1)} %copy-done), kind=kOutput, calls=%fused_computation.6 | convolution fusion | flops 2686451712 | bytes 8126464 | tf_op jit(solution)/shard_map/dot_general | solution.py:150
  201.6 1.4 collective-permute-start.3
  203.0 0.6 fusion.72
  203.6 1.3 compare_select_fusion.2
  205.1 0.6 broadcast_add_fusion
  205.7 7.2 %all-to-all-start = ((s32[8,1,16]{2,1,0:T(1,128)}), s32[8,1,16]{2,1,0:T(1,128)S(1)}, u32[]{:S(2)}, u32[]{:S(2)}) async-start(s32[8,1,16]{2,1,0:T(1,128)} %bitcast.3), calls=%async_computation | async-start | bytes 8192 | tf_op jit(solution)/shard_map/all_to_all | solution.py:92
  213.0 54.5 %all-to-all-done = s32[8,1,16]{2,1,0:T(1,128)S(1)} async-done(((s32[8,1,16]{2,1,0:T(1,128)}), s32[8,1,16]{2,1,0:T(1,128)S(1)}, u32[]{:S(2)}, u32[]{:S(2)}) %all-to-all-start) | async-done | bytes 544 | tf_op jit(solution)/shard_map/all_to_all | solution.py:92
  267.5 0.5 broadcast.239
  268.0 0.7 reduce.7
  268.8 0.2 fusion.64
  269.0 4.9 %fusion.1 = (f32[512]{0:T(512)S(1)}, bf16[512,2048]{1,0:T(8,128)(2,1)}) fusion(bf16[512,2048]{1,0:T(8,128)(2,1)} %collective-permute-done.3, pred[]{:T(512)S(6)} %eq.81, bf16[512,2048]{1,0:T(8,128)(2,1)} %param.27, bf16[128,2048]{1,0:T(8,128)(2,1)} %reduce-scatter.8.cloned.1.call-done, f32[2048]{0:T(1024)S(1)} %convert_element_type.146, s32[128]{0:T(128)S(1)} %eq.71, ...), kind=kOutput, calls=%fused_computation.3 | convolution fusion | flops 275578368 | bytes 6827009 | tf_op jit(solution)/shard_map/dot_general | solution.py:154
  273.9 10.7 %psum.7 = f32[512]{0:T(512)S(1)} all-reduce(f32[512]{0:T(512)S(1)} %get-tuple-element.21), channel_id=1, replica_groups=mesh['section'=2,'dp'=4,'mp'=4] {'mp'}, use_global_device_ids=true, to_apply=%region_12.13 | all-reduce | flops 512 | bytes 4096 | tf_op jit(solution)/shard_map/psum | solution.py:46
  284.5 4.1 %fusion.3 = bf16[512,2048]{1,0:T(8,128)(2,1)} fusion(f32[2048]{0:T(1024)S(1)} %convert_element_type.150, f32[512]{0:T(512)S(1)} %add_rsqrt_fusion, bf16[512,2048]{1,0:T(8,128)(2,1)} %get-tuple-element.22, bf16[512,2048]{1,0:T(8,128)(2,1)} %collective-permute-done.3, pred[]{:T(512)S(6)} %eq.81), kind=kLoop, calls=%fused_computation.5 | loop fusion | flops 5242880 | bytes 6301697 | tf_op jit(solution)/shard_map/convert_element_type | solution.py:164
  (54 shorter events, 0.9 us)
Async XLA Ops:
  7.2 188.2 %copy-start = (bf16[640,2048]{1,0:T(8,128)(2,1)S(1)}, bf16[640,2048]{1,0:T(8,128)(2,1)}, u32[]{:S(2)}) copy-start(bf16[640,2048]{1,0:T(8,128)(2,1)} %param.25) | copy-start | bytes 7864324
  7.2 2.4 copy-start.3
  7.2 59.0 %reduce-scatter.4.cloned.1.call-start = ((), (), s32[]{:S(2)}) async-start(), calls=%async_computation.4 | async-start | bytes 1638400 | tf_op jit(solution)/shard_map/reduce_scatter | solution.py:38
  7.2 1.9 copy-start.1
  13.9 6.0 %copy-start.9 = (s32[2]{0:T(128)S(1)}, s32[2]{0:T(128)}, u32[]{:S(2)}) copy-start(s32[2]{0:T(128)} %param.17) | copy-start | bytes 28
  23.1 2.4 copy-start.12
  33.4 3.8 %copy-start.8 = (s32[128]{0:T(128)S(1)}, s32[128]{0:T(128)}, u32[]{:S(2)}) copy-start(s32[128]{0:T(128)} %param.18) | copy-start | bytes 1540
  33.4 4.4 %copy-start.4 = (bf16[1280]{0:T(1024)(128)(2,1)S(1)}, bf16[1280]{0:T(1024)(128)(2,1)}, u32[]{:S(2)}) copy-start(bf16[1280]{0:T(1024)(128)(2,1)} %param.22) | copy-start | bytes 7684
  33.4 127.3 %reduce-scatter.6.cloned.1.call-start = ((), (), s32[]{:S(2)}) async-start(), calls=%async_computation.5 | async-start | bytes 1638400 | tf_op jit(solution)/shard_map/reduce_scatter | solution.py:38
  66.2 2.4 copy-start.2
  69.6 2.0 collective-permute-start
  73.0 16.9 %collective-permute-start.1 = (bf16[256,1280]{1,0:T(8,128)(2,1)S(1)}, bf16[256,1280]{1,0:T(8,128)(2,1)}, u32[]{:S(2)}, u32[]{:S(2)}) collective-permute-start(bf16[256,1280]{1,0:T(8,128)(2,1)S(1)} %maximum_select_fusion.2), channel_id=1, source_target_pairs={{0,8},{4,12},{8,0},{12,4},{16,24},{20,28},{24,16},{28,20},{1,9},{5... | collective-permute-start | bytes 1966088 | tf_op jit(solution)/shard_map/ppermute | solution.py:16
  92.7 30.3 %collective-permute-start.2 = (bf16[512,1280]{1,0:T(8,128)(2,1)}, bf16[512,1280]{1,0:T(8,128)(2,1)}, u32[]{:S(2)}, u32[]{:S(2)}) collective-permute-start(bf16[512,1280]{1,0:T(8,128)(2,1)} %maximum_select_fusion.1), channel_id=1, source_target_pairs={{0,16},{4,20},{8,24},{12,28},{16,0},{20,4},{24,8},{28,12},{1,17},{... | collective-permute-start | bytes 3932168 | tf_op jit(solution)/shard_map/ppermute | solution.py:16
  125.9 1.4 copy-start.11
  127.3 3.3 %copy-start.7 = (bf16[640]{0:T(1024)(128)(2,1)S(1)}, bf16[640]{0:T(1024)(128)(2,1)}, u32[]{:S(2)}) copy-start(bf16[640]{0:T(1024)(128)(2,1)} %param.24) | copy-start | bytes 3844
  130.6 64.7 %all-gather.2.cloned.1.call-start = ((), (), s32[]{:S(2)}) async-start(), calls=%async_computation.6 | async-start | bytes 1638400 | tf_op jit(solution)/shard_map/all_gather | solution.py:42
  164.0 105.0 %reduce-scatter.8.cloned.1.call-start = ((), (), s32[]{:S(2)}) async-start(), calls=%async_computation.7 | async-start | bytes 4718592 | tf_op jit(solution)/shard_map/reduce_scatter | solution.py:54
  201.6 2.0 copy-start.10
  201.6 11.3 %copy-start.5 = (bf16[2048]{0:T(1024)(128)(2,1)S(1)}, bf16[2048]{0:T(1024)(128)(2,1)}, u32[]{:S(2)}) copy-start(bf16[2048]{0:T(1024)(128)(2,1)} %param.26) | copy-start | bytes 12292
  201.6 11.4 %copy-start.6 = (bf16[2048]{0:T(1024)(128)(2,1)S(1)}, bf16[2048]{0:T(1024)(128)(2,1)}, u32[]{:S(2)}) copy-start(bf16[2048]{0:T(1024)(128)(2,1)} %param.29) | copy-start | bytes 12292
  201.6 67.3 %collective-permute-start.3 = (bf16[512,2048]{1,0:T(8,128)(2,1)}, bf16[512,2048]{1,0:T(8,128)(2,1)}, u32[]{:S(2)}, u32[]{:S(2)}) collective-permute-start(bf16[512,2048]{1,0:T(8,128)(2,1)} %param.28), channel_id=1, source_target_pairs={{0,16},{1,17},{2,18},{3,19},{4,20},{5,21},{6,22},{7,23},{8,24},{9,... | collective-permute-start | bytes 6291464 | tf_op jit(solution)/shard_map/ppermute | solution.py:27
  205.7 61.8 %all-to-all-start = ((s32[8,1,16]{2,1,0:T(1,128)}), s32[8,1,16]{2,1,0:T(1,128)S(1)}, u32[]{:S(2)}, u32[]{:S(2)}) async-start(s32[8,1,16]{2,1,0:T(1,128)} %bitcast.3), calls=%async_computation | async-start | bytes 8192 | tf_op jit(solution)/shard_map/all_to_all | solution.py:92
Sparse Core Ops, SparseCore 0:
  33.6 32.5 reduce-scatter.3
  130.7 30.0 reduce-scatter.5
  164.1 31.1 all-gather.1
  201.7 65.5 reduce-scatter.7
